TPU v7x, 32 devices: a whole 2x2x4 slice. The times are simulated.
32 devices in a mesh: gx: 8 (over z, y), gy: 4 (over x, core).
Axes of the slice: x: 2, y: 2, z: 4, core: 2. Of those that a mesh axis runs over, the one named last changes fastest.
Arguments:
- checkpoint: float32 [16, 32, 1024], P(None, 'gy', 'gx'), may hold values from -6 to 6
- trajectory: float32 [16, 32, 1024], P(None, 'gy', 'gx'), may hold values from -6 to 6
- adjoint_forcing: float32 [16, 32, 1024], P(None, 'gy', 'gx'), may hold values from -6 to 6
- east_diffusion: float32 [16, 32, 1024], P(None, 'gy', 'gx'), may hold values from 0.1 to 1
- north_diffusion: float32 [16, 32, 1024], P(None, 'gy', 'gx'), may hold values from 0.3 to 3
- east_wind: float32 [16, 32, 1024], P(None, 'gy', 'gx'), may hold values from -0.6 to 0.6
- north_wind: float32 [16, 32, 1024], P(None, 'gy', 'gx'), may hold values from -6 to 6, as said below
- level_diffusion: float32 [16], replicated, may hold values from 0.1 to 1
- damping: float32 [16], replicated, may hold values from 0.2 to 2
- source: float32 [16, 32, 1024], P(None, 'gy', 'gx'), may hold values from -4 to 5
- observations: float32 [16, 32, 1024], P(None, 'gy', 'gx'), may hold values from -6 to 6
- observation_weight: float32 [16, 32, 1024], P(None, 'gy', 'gx'), may hold values from 0.1 to 1
- step_index: int32 [1], replicated, may hold values from 0 to 95
Outputs:
- forward_state: float32 [16, 32, 1024], P(None, 'gy', 'gx')
- forward_residual: float32 [16, 32, 1024], P(None, 'gy', 'gx')
- adjoint_state: float32 [16, 32, 1024], P(None, 'gy', 'gx')
Inputs may be any that keep to these rules, and one draw needn't show every extreme that they name: At every face the magnitude of north_wind is at most twice north_diffusion.
All inputs are finite; a program needn't handle non-finite values.
Results may differ from a plain program's by a relative error of at most 0.000091.
Values sent between devices are 32-bit elements; how exact they have to be, the bound alone decides.
A program may use at most 64 MiB of HBM per device.

v0:
```python
import functools
import math

import jax
import jax.numpy as jnp
from jax import lax
from jax.experimental import pallas as pl
from jax.experimental.pallas import tpu as pltpu
from jax.sharding import PartitionSpec as P

OUTER = 2
INNER = 4
DAY_STEPS = 96
RELAXATION = 0.7

FORWARD = 6
FIELDS = 8
CKPT, SOURCE, ED, EW, ND, NW, TRAJ, ADJF = range(FIELDS)

DEPTH = OUTER * INNER + 1
SLOT = DEPTH - 1
GROUP = 32
NINTH = (CKPT, ED, EW)

MESH = pl.DeviceIdType.MESH


def kernel(
    nx,
    ny,
    ckpt_h,
    traj_h,
    adjf_h,
    ed_h,
    nd_h,
    ew_h,
    nw_h,
    level_h,
    damp_h,
    source_h,
    obs_h,
    weight_h,
    step_h,
    state_out,
    resid_out,
    adj_out,
    raw,
    rawx,
    pack_e,
    pack_w,
    recv_e,
    recv_w,
    recvx_e,
    recvx_w,
    coef,
    cf,
    xm,
    x1x,
    x2,
    mu2,
    res,
    fw,
    fg,
    fd,
    fa,
    fb,
    aw,
    ag,
    ad,
    ad2,
    aa,
    ab,
    vert,
    obs_ref,
    weight_ref,
    level_ref,
    damp_ref,
    step_ref,
    load_sem,
    send_lat,
    got_lat,
    send_lon,
    got_lon,
    send_one,
    got_one,
    hello,
):
    levels, rows, lanes = state_out.shape
    wide = INNER
    ring = 2 * rows
    groups = lanes // GROUP
    per = levels // groups
    strips = levels + 2
    tiles = strips + 2 * per
    halo = DEPTH
    kept = GROUP - halo
    gx = lax.axis_index("gx")
    gy = lax.axis_index("gy")
    east = lax.rem(gx + 1, nx)
    west = lax.rem(gx + nx - 1, nx)
    has_n = gy < ny - 1
    has_s = gy > 0
    north = gy + 1
    south = gy - 1
    first_x = gx == 0
    last_x = gx == nx - 1

    inside = pl.ds(1, levels)
    outer = pl.ds(strips, 2 * per)
    main = pl.ds(0, rows)

    order = (ckpt_h, source_h, ed_h, ew_h, nd_h, nw_h, traj_h, adjf_h)
    loads = [
        pltpu.make_async_copy(h, raw.at[f, inside, main, :], load_sem.at[f])
        for f, h in enumerate(order)
    ]
    late_loads = [
        pltpu.make_async_copy(obs_h, obs_ref, load_sem.at[FIELDS]),
        pltpu.make_async_copy(weight_h, weight_ref, load_sem.at[FIELDS + 1]),
    ]
    scalar_loads = [
        pltpu.make_async_copy(level_h, level_ref, load_sem.at[FIELDS + 2]),
        pltpu.make_async_copy(damp_h, damp_ref, load_sem.at[FIELDS + 3]),
        pltpu.make_async_copy(step_h, step_ref, load_sem.at[FIELDS + 4]),
    ]

    barrier = pltpu.get_barrier_semaphore()
    neighbours = (
        (east, gy, True, last_x),
        (west, gy, True, jnp.logical_not(first_x)),
        (gx, north, has_n, False),
        (gx, south, has_s, True),
        (east, north, has_n, last_x),
        (west, north, has_n, jnp.logical_not(first_x)),
        (east, south, has_s, last_x),
        (west, south, has_s, jnp.logical_not(first_x)),
    )
    opposite = (1, 0, 3, 2, 7, 6, 5, 4)

    behind = 0
    for column, row, there, before in neighbours:
        behind = behind + jnp.logical_and(there, before).astype(jnp.int32)

        @pl.when(jnp.logical_and(there, jnp.logical_not(before)))
        def _():
            pl.semaphore_signal(
                barrier, inc=1, device_id={"gx": column, "gy": row}, device_id_type=MESH
            )

    for copy in loads + scalar_loads + late_loads:
        copy.start()

    @pl.when(behind > 0)
    def _():
        pl.semaphore_wait(barrier, behind)

    for k, (column, row, there, before) in enumerate(neighbours):

        @pl.when(jnp.logical_and(there, before))
        def _():
            pl.semaphore_signal(
                hello.at[opposite[k]], inc=1, device_id={"gx": column, "gy": row}, device_id_type=MESH
            )

    def known(*ks):
        for k in ks:
            _, _, there, before = neighbours[k]

            @pl.when(jnp.logical_and(there, jnp.logical_not(before)))
            def _():
                pl.semaphore_wait(hello.at[k], 1)

    def remote(src, dst, send, got, column, row):
        return pltpu.make_async_remote_copy(
            src_ref=src,
            dst_ref=dst,
            send_sem=send,
            recv_sem=got,
            device_id={"gx": column, "gy": row},
            device_id_type=MESH,
        )

    low = pl.ds(0, wide)
    high = pl.ds(rows - wide, wide)
    from_n = pl.ds(rows, wide)
    from_s = pl.ds(ring - wide, wide)
    next_low = pl.ds(wide, 1)
    next_high = pl.ds(rows - wide - 1, 1)
    extra_n = pl.ds(wide - 1, 1)
    extra_s = pl.ds(wide, 1)

    fwd = pl.ds(0, FORWARD)
    adj = pl.ds(FORWARD, FIELDS - FORWARD)
    faces = pl.ds(ND, 2)

    def lat(k, src, dst, column, row):
        return remote(src, dst, send_lat.at[k], got_lat.at[k], column, row)

    up0 = [
        lat(0, raw.at[fwd, inside, high, :], raw.at[fwd, inside, from_s, :], gx, north),
        lat(1, raw.at[faces, inside, next_high, :], rawx.at[:, inside, extra_s, :], gx, north),
        lat(2, raw.at[adj, inside, high, :], raw.at[adj, inside, from_s, :], gx, north),
    ]
    down0 = [
        lat(3, raw.at[fwd, inside, low, :], raw.at[fwd, inside, from_n, :], gx, south),
        lat(4, raw.at[adj, inside, low, :], raw.at[adj, inside, from_n, :], gx, south),
    ]

    def lon(k, src, dst, column, row):
        return remote(src, dst, send_lon.at[k], got_lon.at[k], column, row)

    def lon_copies(k, pack, recv, recvx, column):
        return (
            lon(k, pack, recv.at[:, main, :], column, gy),
            [
                lon(k + 1, pack.at[:, high, :], recv.at[:, from_s, :], column, north),
                lon(k + 2, pack.at[faces, next_high, :], recvx.at[:, extra_s, :], column, north),
            ],
            [lon(k + 3, pack.at[:, low, :], recv.at[:, from_n, :], column, south)],
        )

    lon_e = lon_copies(0, pack_e, recv_w, recvx_w, east)
    lon_w = lon_copies(4, pack_w, recv_e, recvx_e, west)

    def one(k, part):
        def copy(i, src, dst, row):
            return remote(src, dst, send_one.at[k + i], got_one.at[k + i], gx, row)

        return (
            [
                copy(0, xm.at[:, part, high, :], xm.at[:, part, from_s, :], north),
                copy(1, xm.at[0, part, next_high, :], x1x.at[part, extra_s, :], north),
            ],
            [
                copy(2, xm.at[:, part, low, :], xm.at[:, part, from_n, :], south),
                copy(3, xm.at[0, part, next_low, :], x1x.at[part, extra_n, :], south),
            ],
        )

    one_main = one(0, inside)
    one_strips = one(4, outer)

    def start_up(up):
        @pl.when(has_n)
        def _():
            for copy in up:
                copy.start()

    def start_down(down):
        @pl.when(has_s)
        def _():
            for copy in down:
                copy.start()

    def start_lon(copies):
        copies[0].start()
        start_up(copies[1])
        start_down(copies[2])

    def arrive(up, down):
        @pl.when(has_s)
        def _():
            for copy in up:
                copy.wait_recv()

        @pl.when(has_n)
        def _():
            for copy in down:
                copy.wait_recv()

    def flush(up, down):
        @pl.when(has_n)
        def _():
            for copy in up:
                copy.wait_send()

        @pl.when(has_s)
        def _():
            for copy in down:
                copy.wait_send()

    zero_ring = jnp.zeros((ring, lanes), jnp.float32)
    zero_tile = jnp.zeros((rows, lanes), jnp.float32)
    for t in (0, levels + 1):
        raw[CKPT, t] = zero_ring
        for ref in (fa, fb, aa, ab, x2):
            ref[t] = zero_ring
        for k in range(2):
            xm[k, t] = zero_ring

    def clear(part):
        zero = jnp.zeros((wide, lanes), jnp.float32)

        def body(l, carry):
            for f in range(FIELDS):
                raw[f, l + 1, part, :] = zero
            for k in range(2):
                xm[k, l + 1, part, :] = zero
            return carry

        lax.fori_loop(0, levels, body, 0)
        for t in range(strips, tiles):
            for k in range(2):
                xm[k, t, part, :] = zero
        for f in range(FIELDS + 1):
            recv_e[f, part, :] = zero
            recv_w[f, part, :] = zero

    def clear_extra(part):
        zero = jnp.zeros((1, lanes), jnp.float32)
        for t in [*range(1, levels + 1), *range(strips, tiles)]:
            x1x[t, part, :] = zero

    @pl.when(jnp.logical_not(has_n))
    def _():
        clear(from_n)
        clear_extra(extra_n)

    @pl.when(jnp.logical_not(has_s))
    def _():
        clear(from_s)
        clear_extra(extra_s)
        zero = jnp.zeros((1, lanes), jnp.float32)
        for k in range(2):
            for t in range(1, levels + 1):
                rawx[k, t, extra_s, :] = zero
            recvx_e[k, extra_s, :] = zero
            recvx_w[k, extra_s, :] = zero

    for copy in loads:
        copy.wait()
    start_down(down0)

    lane_row = lax.broadcasted_iota(jnp.int32, (rows, lanes), 1)
    lane_ring = lax.broadcasted_iota(jnp.int32, (ring, lanes), 1)
    row_ring = lax.broadcasted_iota(jnp.int32, (ring, lanes), 0)

    def turn(v, shift, axis=1):
        shift = shift % v.shape[axis]
        return pltpu.roll(v, shift, axis) if shift else v

    def choose(place, values):
        out = values[-1]
        for k in range(len(values) - 2, -1, -1):
            out = jnp.where(place == k, values[k], out)
        return out

    def gather(read, place, side, j):
        start = halo if side == 0 else kept
        return choose(place, [turn(read(j + per * g), GROUP * g + start) for g in range(groups)])

    group_row = lane_row // GROUP
    slot_row = (lane_row % GROUP) // SLOT
    nine_row = lane_row % SLOT

    for f in range(FIELDS):
        edge = []
        for side in range(2):
            for j in range(per):
                tile = gather(lambda l: raw[f, l + 1, :rows, :], group_row, side, j)
                raw[f, strips + per * side + j, :rows, :] = tile
                edge.append(tile)
        pack_w[f] = choose(slot_row, [turn(edge[j], SLOT * j - halo) for j in range(per)])
        pack_e[f] = choose(
            slot_row, [turn(edge[per + j], SLOT * j - (kept - SLOT)) for j in range(per)]
        )
    nine_e = [
        choose(
            slot_row,
            [turn(raw[f, strips + per + j, :rows, :], SLOT * j + i - (kept - DEPTH)) for j in range(per)],
        )
        for i, f in enumerate(NINTH)
    ]
    pack_e[FIELDS] = choose(nine_row, nine_e)
    pack_w[FIELDS] = choose(
        slot_row, [turn(raw[CKPT, strips + j, :rows, :], SLOT * j - (halo + SLOT)) for j in range(per)]
    )

    @pl.when(last_x)
    def _():
        start_lon(lon_e)

    @pl.when(jnp.logical_not(first_x))
    def _():
        start_lon(lon_w)

    known(2)
    start_up(up0)

    @pl.when(jnp.logical_not(last_x))
    def _():
        known(0, 4, 6)
        start_lon(lon_e)

    for copy in scalar_loads:
        copy.wait()

    total_lanes = lanes * nx

    def heat_of(column):
        column = gx * lanes + column
        column = jnp.where(column < 0, column + total_lanes, column)
        column = jnp.where(column >= total_lanes, column - total_lanes, column)
        phase = (
            2.0 * math.pi * column.astype(jnp.float32) / total_lanes
            - 2.0 * math.pi * step_ref[0].astype(jnp.float32) / DAY_STEPS
        )
        return jnp.cos(phase)

    lane_one = lax.broadcasted_iota(jnp.int32, (1, lanes), 1)
    heat_main = heat_of(lane_one)
    heat_side = (
        heat_of(lane_one % GROUP - halo),
        heat_of(lane_one % GROUP + (lanes - kept)),
    )
    row_global = gy * rows + jnp.where(row_ring < rows + wide, row_ring, row_ring - ring)
    open_face = (row_global >= 0) & (row_global < rows * ny - 1)

    def level_terms(l):
        up = jnp.where(l < levels - 1, level_ref[l], 0.0)
        down = jnp.where(l > 0, level_ref[jnp.maximum(l - 1, 0)], 0.0)
        return up, down, damp_ref[l]

    group_one = lane_ring // GROUP
    for j in range(per):
        terms = [level_terms(j + per * g) for g in range(groups)]
        for k in range(3):
            vert[k, j] = choose(group_one, [jnp.full((ring, lanes), term[k]) for term in terms])

    class Main:
        def __init__(self, l):
            self.t = l + 1
            self.l = l
            self.heat = heat_main

        def terms(self):
            return level_terms(self.l)

        def above(self, ref):
            return ref[self.t + 1]

        def below(self, ref):
            return ref[self.t - 1]

    class Strip:
        def __init__(self, k):
            self.t = strips + k
            self.j = k % per
            self.base = strips + k - self.j
            self.heat = heat_side[k // per]

        def terms(self):
            return vert[0, self.j], vert[1, self.j], vert[2, self.j]

        def above(self, ref):
            if self.j < per - 1:
                return ref[self.t + 1]
            return turn(ref[self.base], -GROUP)

        def below(self, ref):
            if self.j > 0:
                return ref[self.t - 1]
            return turn(ref[self.base + per - 1], GROUP)

    def each_main(body):
        def step(l, carry):
            body(Main(l))
            return carry

        lax.fori_loop(0, levels, step, 0, unroll=True)

    def each_strip(body):
        for k in range(2 * per):
            body(Strip(k))

    def off_forward(c, ref, extra=None):
        up, down, _ = c.terms()
        v = ref[c.t]
        above = turn(v, -1, 0)
        below = turn(v, 1, 0)
        if extra is not None:
            more = jnp.concatenate([extra[c.t], extra[c.t]], axis=0)
            above = jnp.where(row_ring == rows + wide - 1, more, above)
            below = jnp.where(row_ring == rows + wide, more, below)
        off = (
            turn(v, -1) * coef[1, c.t]
            - turn(v, 1) * coef[2, c.t]
            + above * coef[5, c.t]
            - below * coef[6, c.t]
            - up * c.above(ref)
            - down * c.below(ref)
        )
        return v, off

    def off_adjoint(c, ref):
        up, down, _ = c.terms()
        v = ref[c.t]
        off = (
            turn(v, 1) * coef[3, c.t]
            - turn(v, -1) * coef[0, c.t]
            + turn(v, 1, 0) * coef[7, c.t]
            - turn(v, -1, 0) * coef[4, c.t]
            - up * c.above(ref)
            - down * c.below(ref)
        )
        return v, off

    def resid_forward(c, ref, extra=None):
        _, _, damp = c.terms()
        x, off = off_forward(c, ref, extra)
        t = jnp.tanh(x)
        local = damp * (1.0 - t * t)
        diag = coef[8, c.t]
        r = x * diag + off + damp * t - cf[c.t]
        w = RELAXATION / (coef[9, c.t] + local)
        d = -w * r
        fw[c.t] = w
        fg[c.t] = 1.0 - w * (diag + local)
        fd[c.t] = d
        fa[c.t] = d

    def resid_adjoint(c, ref):
        m, off = off_adjoint(c, ref)
        d = ad[c.t] - (1.0 - ag[c.t]) * m - aw[c.t] * off
        ad2[c.t] = d
        aa[c.t] = d

    def lin_forward(c, src):
        v, off = off_forward(c, src)
        return fg[c.t] * v + fd[c.t] - fw[c.t] * off

    def lin_adjoint(c, src, base):
        v, off = off_adjoint(c, src)
        return ag[c.t] * v + base[c.t] - aw[c.t] * off

    def prepare(c):
        up, down, damp = c.terms()
        de = raw[ED, c.t]
        fe = 0.5 * raw[EW, c.t]
        dn = jnp.where(open_face, raw[ND, c.t], 0.0)
        fn = jnp.where(open_face, 0.5 * raw[NW, c.t], 0.0)
        dnx = rawx[0, c.t]
        fnx = 0.5 * rawx[1, c.t]
        anx, bnx = fnx + dnx, fnx - dnx
        a, b = fe + de, fe - de
        an, bn = fn + dn, fn - dn
        a_w = turn(a, 1)
        b_w = turn(b, 1)
        last = row_ring == rows + wide
        an_s = jnp.where(last, jnp.concatenate([anx, anx], axis=0), turn(an, 1, 0))
        bn_s = jnp.where(last, jnp.concatenate([bnx, bnx], axis=0), turn(bn, 1, 0))
        diag = 1.0 + (a - b_w) + (an - bn_s) + (up + down)
        total = 1.0 + de + 0.5 * (a_w - b_w) + dn + 0.5 * (an_s - bn_s) + (up + down)
        for k, value in enumerate((a, b, a_w, b_w, an, bn, an_s, bn_s, diag, total)):
            coef[k, c.t] = value
        cf[c.t] = raw[CKPT, c.t] + raw[SOURCE, c.t] * c.heat
        t = jnp.tanh(raw[TRAJ, c.t])
        local = damp * (1.0 - t * t)
        w = RELAXATION / (total + local)
        start_delta = w * raw[ADJF, c.t]
        aw[c.t] = w
        ag[c.t] = 1.0 - w * (diag + local)
        ad[c.t] = start_delta
        aa[c.t] = start_delta
        resid_forward(c, raw.at[CKPT])

    pairs = ((fa, fb, aa, ab), (fb, fa, ab, aa))
    last = pairs[(INNER - 2) % 2]

    def sweeps(each, base):
        for k in range(INNER - 2):
            f_src, f_dst, a_src, a_dst = pairs[k % 2]

            def body(c):
                f_dst[c.t] = lin_forward(c, f_src)
                a_dst[c.t] = lin_adjoint(c, a_src, base)

            each(body)

    def close1(c):
        xm[0, c.t, :rows, :] = raw[CKPT, c.t, :rows, :] + lin_forward(c, last[0])[:rows]
        xm[1, c.t, :rows, :] = lin_adjoint(c, last[2], ad)[:rows]

    def second(c):
        resid_forward(c, xm.at[0], x1x)
        resid_adjoint(c, xm.at[1])

    def close2(c):
        x2[c.t] = xm[0, c.t] + lin_forward(c, last[0])
        mu2[c.t] = xm[1, c.t, :rows, :] + lin_adjoint(c, last[2], ad2)[:rows]

    def finish(c):
        _, _, damp = c.terms()
        x, off = off_forward(c, x2)
        r = x * coef[8, c.t] + off + damp * jnp.tanh(x) - cf[c.t]
        res[c.t] = r[:rows]

    @pl.when(first_x)
    def _():
        known(1, 5, 7)
        start_lon(lon_w)

    arrive(up0, down0)
    each_main(prepare)
    sweeps(each_main, ad)
    each_main(close1)
    start_up(one_main[0])
    start_down(one_main[1])

    spot = lane_ring % GROUP
    from_w = (spot > 0) & (spot < halo)
    from_e = (spot >= kept) & (spot < GROUP - 1)
    spot_row = spot[:rows]
    for f in range(FIELDS):
        for side in range(2):
            for j in range(per):
                raw[f, strips + per * side + j, rows:, :] = gather(
                    lambda l: raw[f, l + 1, rows:, :], group_row, side, j
                )
    for copies in (lon_e, lon_w):
        copies[0].wait_recv()
        arrive(copies[1], copies[2])

    for f in range(FIELDS):
        for j in range(per):
            t = strips + j
            tile = jnp.where(from_w, turn(recv_w[f], 1 - SLOT * j), raw[f, t])
            if f in NINTH:
                nine = turn(recv_w[FIELDS], -(SLOT * j + NINTH.index(f)))
                tile = jnp.where(spot == 0, nine, tile)
            raw[f, t] = tile
            t = strips + per + j
            tile = jnp.where(from_e, turn(recv_e[f], kept - SLOT * j), raw[f, t])
            if f == CKPT:
                nine = turn(recv_e[FIELDS], GROUP - 1 - SLOT * j)
                tile = jnp.where(spot == GROUP - 1, nine, tile)
            raw[f, t] = tile
    for k in range(2):
        for j in range(per):
            for side, (recvx, shift, where) in enumerate(
                ((recvx_w, 1 - SLOT * j, from_w), (recvx_e, kept - SLOT * j, from_e))
            ):
                t = strips + per * side + j
                tile = gather(lambda l: rawx[k, l + 1], group_row, side, j)
                rawx[k, t] = jnp.where(where[:rows], turn(recvx[k], shift), tile)

    each_strip(prepare)
    sweeps(each_strip, ad)
    each_strip(close1)
    start_up(one_strips[0])
    start_down(one_strips[1])

    arrive(*one_main)
    each_main(second)
    sweeps(each_main, ad2)
    each_main(close2)
    each_main(finish)

    arrive(*one_strips)
    each_strip(second)
    sweeps(each_strip, ad2)
    each_strip(close2)
    each_strip(finish)

    for copy in late_loads:
        copy.wait()

    west_edge = lane_row < DEPTH
    east_edge = lane_row >= lanes - DEPTH

    def merged(ref, l):
        j, g = l % per, l // per
        w = turn(ref[strips + j][:rows], -(GROUP * g + halo))
        e = turn(ref[strips + per + j][:rows], lanes - kept - GROUP * g)
        return jnp.where(west_edge, w, jnp.where(east_edge, e, ref[l + 1][:rows]))

    for l in range(levels):
        x = merged(x2, l)
        state_out[l] = x
        adj_out[l] = merged(mu2, l) + weight_ref[l] * (x - obs_ref[l])
        resid_out[l] = merged(res, l)

    flush(up0, down0)
    flush(*one_main)
    flush(*one_strips)
    for copies in (lon_e, lon_w):
        copies[0].wait_send()
        flush(copies[1], copies[2])


def hand_over(a, b, c, x, y, z, sem):
    gives = [
        pltpu.make_async_copy(held, ref, sem.at[k])
        for k, (held, ref) in enumerate(((a, x), (b, y), (c, z)))
    ]
    for copy in gives:
        copy.start()
    for copy in gives:
        copy.wait()


def solution(mesh):
    nx, ny = mesh.shape["gx"], mesh.shape["gy"]

    def per_device(*arrays):
        levels, rows, lanes = arrays[0].shape
        groups = lanes // GROUP
        assert rows >= 2 * INNER and rows >= INNER + 1 and levels % groups == 0 and nx > 2
        per = levels // groups
        assert per * SLOT <= GROUP and GROUP >= 3 * DEPTH and len(NINTH) <= SLOT
        ring = 2 * rows
        tiles = levels + 2 + 2 * per
        f32 = jnp.float32
        out = jax.ShapeDtypeStruct((levels, rows, lanes), f32)
        hbm = pl.BlockSpec(memory_space=pltpu.HBM)
        vmem = pl.BlockSpec(memory_space=pltpu.VMEM)

        def buf(*shape):
            return pltpu.VMEM(shape, f32)

        def full():
            return buf(tiles, ring, lanes)

        def dma(n):
            return pltpu.SemaphoreType.DMA((n,))

        results = pl.pallas_call(
            functools.partial(kernel, nx, ny),
            name="step_pair",
            out_shape=(pltpu.VMEM(out.shape, f32),) * 3,
            in_specs=[hbm] * 13,
            out_specs=(vmem,) * 3,
            scratch_shapes=[
                buf(FIELDS, tiles, ring, lanes),
                buf(2, tiles, rows, lanes),
                buf(FIELDS + 1, rows, lanes),
                buf(FIELDS + 1, rows, lanes),
                buf(FIELDS + 1, ring, lanes),
                buf(FIELDS + 1, ring, lanes),
                buf(2, rows, lanes),
                buf(2, rows, lanes),
                buf(10, tiles, ring, lanes),
                full(),
                buf(2, tiles, ring, lanes),
                buf(tiles, rows, lanes),
                full(),
                buf(tiles, rows, lanes),
                buf(tiles, rows, lanes),
            ]
            + [full() for _ in range(11)]
            + [
                buf(3, per, ring, lanes),
                buf(levels, rows, lanes),
                buf(levels, rows, lanes),
                pltpu.SMEM((levels,), f32),
                pltpu.SMEM((levels,), f32),
                pltpu.SMEM((1,), jnp.int32),
                dma(FIELDS + 5),
                dma(5),
                dma(5),
                dma(8),
                dma(8),
                dma(8),
                dma(8),
                pltpu.SemaphoreType.REGULAR((8,)),
            ],
            compiler_params=pltpu.CompilerParams(
                collective_id=0, has_side_effects=True, vmem_limit_bytes=67043328 - 3 * 4 * math.prod(out.shape)
            ),
        )(*arrays)
        return pl.pallas_call(
            hand_over,
            name="hand_over",
            out_shape=(out, out, out),
            in_specs=[vmem] * 3,
            out_specs=(hbm, hbm, hbm),
            scratch_shapes=[dma(3)],
            compiler_params=pltpu.CompilerParams(vmem_limit_bytes=4 * 2**20),
        )(*results)

    block = P(None, "gy", "gx")
    return jax.shard_map(
        per_device,
        mesh=mesh,
        in_specs=(block,) * 7 + (P(), P(), block, block, block, P()),
        out_specs=(block,) * 3,
        check_vma=False,
    )
```

profile of v0, /device:TPU:1, one launch (start us, length us, event | category | flops | bytes accessed | tf_op | source)
XLA Modules:
  0.0 17.2 jit_solution(1640977821955954516)
XLA Ops:
  1.3 15.2 %step_pair.1 = (f32[16,8,128]{2,1,0:T(8,128)S(1)}, f32[16,8,128]{2,1,0:T(8,128)S(1)}, f32[16,8,128]{2,1,0:T(8,128)S(1)}) custom-call(f32[16,8,128]{2,1,0:T(8,128)} %ckpt_h.1, f32[16,8,128]{2,1,0:T(8,128)} %traj_h.1, f32[16,8,128]{2,1,0:T(8,128)} %adjf_h.1, f32[16,8,128]{2,1,0:T(8,128)} %ed_h.1, f32[16,8,128]{2,1,0:T(8,128)} %nd_h.1, f32[16,8,128]{2,1,0:T(8,128)} %ew_h.1, ...), custom_call_target="tpu_custom_call" | custom-call | tf_op jit(solution)/shard_map/step_pair/pallas_call | solution.py:727
  16.5 0.7 %hand_over.1 = (f32[16,8,128]{2,1,0:T(8,128)}, f32[16,8,128]{2,1,0:T(8,128)}, f32[16,8,128]{2,1,0:T(8,128)}) custom-call(f32[16,8,128]{2,1,0:T(8,128)S(1)} %get-tuple-element.6.a, f32[16,8,128]{2,1,0:T(8,128)S(1)} %get-tuple-element.7.b, f32[16,8,128]{2,1,0:T(8,128)S(1)} %get-tuple-element.8.c), custom_call_target="tpu_custom_call" | custom-call | tf_op jit(solution)/shard_map/hand_over/pallas_call | solution.py:771
where the time goes:
time: 17.3 us; the launch traced here: 17.2 us
  Pallas kernels  15.9 us (92%)
  between operations  1.29 us (7%)
    pallas_call x1, Pallas kernels, per_device(): pl.pallas_call(functools.partial(kernel, nx, ny), name='step_pair', out_s...  15.2 us
    pallas_call x1, Pallas kernels, per_device(): pl.pallas_call(hand_over, name='hand_over', out_shape=(out, out, out), in...  0.7 us

commit v1 on v0

--- a/solution.py
+++ b/solution.py
@@ -106,7 +106,6 @@
     last_x = gx == nx - 1
 
     inside = pl.ds(1, levels)
-    outer = pl.ds(strips, 2 * per)
     main = pl.ds(0, rows)
 
     order = (ckpt_h, source_h, ed_h, ew_h, nd_h, nw_h, traj_h, adjf_h)
@@ -125,15 +124,23 @@
     ]
 
     barrier = pltpu.get_barrier_semaphore()
+    odd_x = lax.rem(gx, 2) == 1
+    odd_y = lax.rem(gy, 2) == 1
+    even_y = jnp.logical_not(odd_y)
+    inner_x = jnp.logical_not(first_x)
+    before_e = jnp.logical_or(last_x, odd_x)
+    before_w = jnp.logical_and(inner_x, odd_x)
+    before_de = jnp.logical_or(last_x, even_y)
+    before_dw = jnp.logical_and(inner_x, even_y)
     neighbours = (
-        (east, gy, True, last_x),
-        (west, gy, True, jnp.logical_not(first_x)),
-        (gx, north, has_n, False),
-        (gx, south, has_s, True),
-        (east, north, has_n, last_x),
-        (west, north, has_n, jnp.logical_not(first_x)),
-        (east, south, has_s, last_x),
-        (west, south, has_s, jnp.logical_not(first_x)),
+        (east, gy, True, before_e),
+        (west, gy, True, before_w),
+        (gx, north, has_n, odd_y),
+        (gx, south, has_s, odd_y),
+        (east, north, has_n, before_de),
+        (west, north, has_n, before_dw),
+        (east, south, has_s, before_de),
+        (west, south, has_s, before_dw),
     )
     opposite = (1, 0, 3, 2, 7, 6, 5, 4)
 
@@ -238,7 +245,6 @@
         )
 
     one_main = one(0, inside)
-    one_strips = one(4, outer)
 
     def start_up(up):
         @pl.when(has_n)
@@ -329,7 +335,17 @@
 
     for copy in loads:
         copy.wait()
-    start_down(down0)
+
+    def send_lat():
+        known(2)
+        start_up(up0)
+        known(3)
+        start_down(down0)
+
+    @pl.when(jnp.logical_not(last_x))
+    def _():
+        send_lat()
+
 
     lane_row = lax.broadcasted_iota(jnp.int32, (rows, lanes), 1)
     lane_ring = lax.broadcasted_iota(jnp.int32, (ring, lanes), 1)
@@ -350,47 +366,53 @@
         return choose(place, [turn(read(j + per * g), GROUP * g + start) for g in range(groups)])
 
     group_row = lane_row // GROUP
-    slot_row = (lane_row % GROUP) // SLOT
     nine_row = lane_row % SLOT
 
+    def slots(f, shift, turns=(0,)):
+        rolled = [turn(raw[f, level_of(k) + 1, :rows, :], SLOT * k + shift) for k in range(levels)]
+        return [choose((lane_row // SLOT + move) % levels, rolled) for move in turns]
+
+    def level_of(k):
+        return k % per + per * (k // per)
+
+    nine = None
     for f in range(FIELDS):
-        edge = []
-        for side in range(2):
-            for j in range(per):
-                tile = gather(lambda l: raw[f, l + 1, :rows, :], group_row, side, j)
-                raw[f, strips + per * side + j, :rows, :] = tile
-                edge.append(tile)
-        pack_w[f] = choose(slot_row, [turn(edge[j], SLOT * j - halo) for j in range(per)])
-        pack_e[f] = choose(
-            slot_row, [turn(edge[per + j], SLOT * j - (kept - SLOT)) for j in range(per)]
-        )
-    nine_e = [
-        choose(
-            slot_row,
-            [turn(raw[f, strips + per + j, :rows, :], SLOT * j + i - (kept - DEPTH)) for j in range(per)],
-        )
-        for i, f in enumerate(NINTH)
-    ]
-    pack_e[FIELDS] = choose(nine_row, nine_e)
-    pack_w[FIELDS] = choose(
-        slot_row, [turn(raw[CKPT, strips + j, :rows, :], SLOT * j - (halo + SLOT)) for j in range(per)]
-    )
+        if f in NINTH:
+            pack_e[f], beside = slots(f, SLOT, (0, 1))
+            i = NINTH.index(f)
+            beside = turn(beside, -i)
+            nine = beside if nine is None else jnp.where(nine_row == SLOT - 1 - i, beside, nine)
+        else:
+            (pack_e[f],) = slots(f, SLOT)
+    pack_e[FIELDS] = nine
 
     @pl.when(last_x)
     def _():
         start_lon(lon_e)
-
-    @pl.when(jnp.logical_not(first_x))
+        send_lat()
+
+    for f in range(FIELDS):
+        if f == CKPT:
+            pack_w[f], pack_w[FIELDS] = slots(f, 0, (0, -1))
+        else:
+            (pack_w[f],) = slots(f, 0)
+
+    @pl.when(inner_x)
     def _():
+        known(1, 5, 7)
         start_lon(lon_w)
-
-    known(2)
-    start_up(up0)
 
     @pl.when(jnp.logical_not(last_x))
     def _():
         known(0, 4, 6)
         start_lon(lon_e)
+
+    for f in range(FIELDS):
+        for side in range(2):
+            for j in range(per):
+                raw[f, strips + per * side + j, :rows, :] = gather(
+                    lambda l: raw[f, l + 1, :rows, :], group_row, side, j
+                )
 
     for copy in scalar_loads:
         copy.wait()
@@ -469,9 +491,9 @@
 
         lax.fori_loop(0, levels, step, 0, unroll=True)
 
-    def each_strip(body):
-        for k in range(2 * per):
-            body(Strip(k))
+    def each_strip(side, body):
+        for j in range(per):
+            body(Strip(per * side + j))
 
     def off_forward(c, ref, extra=None):
         up, down, _ = c.terms()
@@ -617,38 +639,38 @@
                 raw[f, strips + per * side + j, rows:, :] = gather(
                     lambda l: raw[f, l + 1, rows:, :], group_row, side, j
                 )
-    for copies in (lon_e, lon_w):
+    for k in range(2):
+        for side in range(2):
+            for j in range(per):
+                rawx[k, strips + per * side + j] = gather(lambda l: rawx[k, l + 1], group_row, side, j)
+    def unpack(side):
+        recv, recvx, where, lead, nines = (
+            (recv_w, recvx_w, from_w, 1, NINTH),
+            (recv_e, recvx_e, from_e, kept, (CKPT,)),
+        )[side]
+        beyond = spot == (0 if side == 0 else GROUP - 1)
+        for j in range(per):
+            t = strips + per * side + j
+            shift = lead - SLOT * j
+            for f in range(FIELDS):
+                tile = jnp.where(where, turn(recv[f], shift), raw[f, t])
+                if f in nines:
+                    tile = jnp.where(beyond, turn(recv[FIELDS], shift + nines.index(f)), tile)
+                raw[f, t] = tile
+            for k in range(2):
+                rawx[k, t] = jnp.where(where[:rows], turn(recvx[k], shift), rawx[k, t])
+
+    one_strips = (one(4, pl.ds(strips, per)), one(8, pl.ds(strips + per, per)))
+    for side, copies in ((1, lon_w), (0, lon_e)):
         copies[0].wait_recv()
         arrive(copies[1], copies[2])
-
-    for f in range(FIELDS):
-        for j in range(per):
-            t = strips + j
-            tile = jnp.where(from_w, turn(recv_w[f], 1 - SLOT * j), raw[f, t])
-            if f in NINTH:
-                nine = turn(recv_w[FIELDS], -(SLOT * j + NINTH.index(f)))
-                tile = jnp.where(spot == 0, nine, tile)
-            raw[f, t] = tile
-            t = strips + per + j
-            tile = jnp.where(from_e, turn(recv_e[f], kept - SLOT * j), raw[f, t])
-            if f == CKPT:
-                nine = turn(recv_e[FIELDS], GROUP - 1 - SLOT * j)
-                tile = jnp.where(spot == GROUP - 1, nine, tile)
-            raw[f, t] = tile
-    for k in range(2):
-        for j in range(per):
-            for side, (recvx, shift, where) in enumerate(
-                ((recvx_w, 1 - SLOT * j, from_w), (recvx_e, kept - SLOT * j, from_e))
-            ):
-                t = strips + per * side + j
-                tile = gather(lambda l: rawx[k, l + 1], group_row, side, j)
-                rawx[k, t] = jnp.where(where[:rows], turn(recvx[k], shift), tile)
-
-    each_strip(prepare)
-    sweeps(each_strip, ad)
-    each_strip(close1)
-    start_up(one_strips[0])
-    start_down(one_strips[1])
+        unpack(side)
+        each = functools.partial(each_strip, side)
+        each(prepare)
+        sweeps(each, ad)
+        each(close1)
+        start_up(one_strips[side][0])
+        start_down(one_strips[side][1])
 
     arrive(*one_main)
     each_main(second)
@@ -656,11 +678,13 @@
     each_main(close2)
     each_main(finish)
 
-    arrive(*one_strips)
-    each_strip(second)
-    sweeps(each_strip, ad2)
-    each_strip(close2)
-    each_strip(finish)
+    for side in (1, 0):
+        arrive(*one_strips[side])
+        each = functools.partial(each_strip, side)
+        each(second)
+        sweeps(each, ad2)
+        each(close2)
+        each(finish)
 
     for copy in late_loads:
         copy.wait()
@@ -682,7 +706,8 @@
 
     flush(up0, down0)
     flush(*one_main)
-    flush(*one_strips)
+    for copies in one_strips:
+        flush(*copies)
     for copies in (lon_e, lon_w):
         copies[0].wait_send()
         flush(copies[1], copies[2])
@@ -760,8 +785,8 @@
                 dma(5),
                 dma(8),
                 dma(8),
-                dma(8),
-                dma(8),
+                dma(12),
+                dma(12),
                 pltpu.SemaphoreType.REGULAR((8,)),
             ],
             compiler_params=pltpu.CompilerParams(

time: 17.3 us -> 16.4 us (0.948)
  Pallas kernels: 15.9 us -> 14.9 us
    pallas_call x1, Pallas kernels: 15.2 us -> 14.2 us  [per_device(): pl.pallas_call(functools.partial(kernel, nx, ny), name='step_pair', out_s...]
where the time goes in v1:
time: 16.4 us; the launch traced here: 16.2 us
  Pallas kernels  14.9 us (91%)
  between operations  1.29 us (8%)
    pallas_call x1, Pallas kernels, per_device(): pl.pallas_call(functools.partial(kernel, nx, ny), name='step_pair', out_s...  14.2 us
    pallas_call x1, Pallas kernels, per_device(): pl.pallas_call(hand_over, name='hand_over', out_shape=(out, out, out), in...  0.7 us

profile of v1, /device:TPU:1, one launch (start us, length us, event | category | flops | bytes accessed | tf_op | source)
XLA Modules:
  0.0 16.2 jit_solution(10304785195581706438)
XLA Ops:
  1.3 14.2 %step_pair.1 = (f32[16,8,128]{2,1,0:T(8,128)S(1)}, f32[16,8,128]{2,1,0:T(8,128)S(1)}, f32[16,8,128]{2,1,0:T(8,128)S(1)}) custom-call(f32[16,8,128]{2,1,0:T(8,128)} %ckpt_h.1, f32[16,8,128]{2,1,0:T(8,128)} %traj_h.1, f32[16,8,128]{2,1,0:T(8,128)} %adjf_h.1, f32[16,8,128]{2,1,0:T(8,128)} %ed_h.1, f32[16,8,128]{2,1,0:T(8,128)} %nd_h.1, f32[16,8,128]{2,1,0:T(8,128)} %ew_h.1, ...), custom_call_target="tpu_custom_call" | custom-call | tf_op jit(solution)/shard_map/step_pair/pallas_call | solution.py:752
  15.5 0.7 %hand_over.1 = (f32[16,8,128]{2,1,0:T(8,128)}, f32[16,8,128]{2,1,0:T(8,128)}, f32[16,8,128]{2,1,0:T(8,128)}) custom-call(f32[16,8,128]{2,1,0:T(8,128)S(1)} %get-tuple-element.6.a, f32[16,8,128]{2,1,0:T(8,128)S(1)} %get-tuple-element.7.b, f32[16,8,128]{2,1,0:T(8,128)S(1)} %get-tuple-element.8.c), custom_call_target="tpu_custom_call" | custom-call | tf_op jit(solution)/shard_map/hand_over/pallas_call | solution.py:796

commit v2 on v1

--- a/solution.py
+++ b/solution.py
@@ -13,7 +13,6 @@
 DAY_STEPS = 96
 RELAXATION = 0.7
 
-FORWARD = 6
 FIELDS = 8
 CKPT, SOURCE, ED, EW, ND, NW, TRAJ, ADJF = range(FIELDS)
 
@@ -71,18 +70,14 @@
     aa,
     ab,
     vert,
-    obs_ref,
-    weight_ref,
+    late_ref,
+    bytes_ref,
     level_ref,
     damp_ref,
     step_ref,
     load_sem,
-    send_lat,
-    got_lat,
-    send_lon,
-    got_lon,
-    send_one,
-    got_one,
+    send,
+    got,
     hello,
 ):
     levels, rows, lanes = state_out.shape
@@ -110,17 +105,17 @@
 
     order = (ckpt_h, source_h, ed_h, ew_h, nd_h, nw_h, traj_h, adjf_h)
     loads = [
-        pltpu.make_async_copy(h, raw.at[f, inside, main, :], load_sem.at[f])
+        pltpu.make_async_copy(h, raw.at[f, inside, main, :], load_sem.at[0])
         for f, h in enumerate(order)
     ]
     late_loads = [
-        pltpu.make_async_copy(obs_h, obs_ref, load_sem.at[FIELDS]),
-        pltpu.make_async_copy(weight_h, weight_ref, load_sem.at[FIELDS + 1]),
+        pltpu.make_async_copy(obs_h, late_ref.at[0], load_sem.at[1]),
+        pltpu.make_async_copy(weight_h, late_ref.at[1], load_sem.at[1]),
     ]
     scalar_loads = [
-        pltpu.make_async_copy(level_h, level_ref, load_sem.at[FIELDS + 2]),
-        pltpu.make_async_copy(damp_h, damp_ref, load_sem.at[FIELDS + 3]),
-        pltpu.make_async_copy(step_h, step_ref, load_sem.at[FIELDS + 4]),
+        pltpu.make_async_copy(level_h, level_ref, load_sem.at[2]),
+        pltpu.make_async_copy(damp_h, damp_ref, load_sem.at[3]),
+        pltpu.make_async_copy(step_h, step_ref, load_sem.at[4]),
     ]
 
     barrier = pltpu.get_barrier_semaphore()
@@ -142,7 +137,7 @@
         (east, south, has_s, before_de),
         (west, south, has_s, before_dw),
     )
-    opposite = (1, 0, 3, 2, 7, 6, 5, 4)
+    answer_to = (1, 0, 3, 2, 1, 0, 1, 0)
 
     behind = 0
     for column, row, there, before in neighbours:
@@ -166,16 +161,25 @@
         @pl.when(jnp.logical_and(there, before))
         def _():
             pl.semaphore_signal(
-                hello.at[opposite[k]], inc=1, device_id={"gx": column, "gy": row}, device_id_type=MESH
+                hello.at[answer_to[k]], inc=1, device_id={"gx": column, "gy": row}, device_id_type=MESH
             )
 
-    def known(*ks):
+    def known(side, *ks):
+        count = 0
         for k in ks:
             _, _, there, before = neighbours[k]
-
-            @pl.when(jnp.logical_and(there, jnp.logical_not(before)))
-            def _():
-                pl.semaphore_wait(hello.at[k], 1)
+            count = count + jnp.logical_and(there, jnp.logical_not(before)).astype(jnp.int32)
+
+        @pl.when(count > 0)
+        def _():
+            pl.semaphore_wait(hello.at[side], count)
+
+    def wait_rows(n, sem):
+        part = bytes_ref.at[pl.ds(0, n), :]
+        pltpu.make_async_copy(part, part, sem).wait()
+
+    def rows_of(copies):
+        return sum(math.prod(copy.src_ref.shape) for copy in copies) // lanes
 
     def remote(src, dst, send, got, column, row):
         return pltpu.make_async_remote_copy(
@@ -196,55 +200,61 @@
     extra_n = pl.ds(wide - 1, 1)
     extra_s = pl.ds(wide, 1)
 
-    fwd = pl.ds(0, FORWARD)
-    adj = pl.ds(FORWARD, FIELDS - FORWARD)
     faces = pl.ds(ND, 2)
 
-    def lat(k, src, dst, column, row):
-        return remote(src, dst, send_lat.at[k], got_lat.at[k], column, row)
-
     up0 = [
-        lat(0, raw.at[fwd, inside, high, :], raw.at[fwd, inside, from_s, :], gx, north),
-        lat(1, raw.at[faces, inside, next_high, :], rawx.at[:, inside, extra_s, :], gx, north),
-        lat(2, raw.at[adj, inside, high, :], raw.at[adj, inside, from_s, :], gx, north),
+        remote(raw.at[:, inside, high, :], raw.at[:, inside, from_s, :], send.at[0], got.at[0], gx, north),
+        remote(
+            raw.at[faces, inside, next_high, :], rawx.at[:, inside, extra_s, :], send.at[0], got.at[0], gx, north
+        ),
     ]
     down0 = [
-        lat(3, raw.at[fwd, inside, low, :], raw.at[fwd, inside, from_n, :], gx, south),
-        lat(4, raw.at[adj, inside, low, :], raw.at[adj, inside, from_n, :], gx, south),
+        remote(raw.at[:, inside, low, :], raw.at[:, inside, from_n, :], send.at[1], got.at[1], gx, south)
     ]
-
-    def lon(k, src, dst, column, row):
-        return remote(src, dst, send_lon.at[k], got_lon.at[k], column, row)
 
     def lon_copies(k, pack, recv, recvx, column):
         return (
-            lon(k, pack, recv.at[:, main, :], column, gy),
+            [remote(pack, recv.at[:, main, :], send.at[2], got.at[k], column, gy)],
             [
-                lon(k + 1, pack.at[:, high, :], recv.at[:, from_s, :], column, north),
-                lon(k + 2, pack.at[faces, next_high, :], recvx.at[:, extra_s, :], column, north),
+                remote(
+                    pack.at[:, high, :], recv.at[:, from_s, :], send.at[0], got.at[k + 1], column, north
+                ),
+                remote(
+                    pack.at[faces, next_high, :],
+                    recvx.at[:, extra_s, :],
+                    send.at[0],
+                    got.at[k + 1],
+                    column,
+                    north,
+                ),
             ],
-            [lon(k + 3, pack.at[:, low, :], recv.at[:, from_n, :], column, south)],
+            [
+                remote(
+                    pack.at[:, low, :], recv.at[:, from_n, :], send.at[1], got.at[k + 2], column, south
+                )
+            ],
         )
 
-    lon_e = lon_copies(0, pack_e, recv_w, recvx_w, east)
-    lon_w = lon_copies(4, pack_w, recv_e, recvx_e, west)
+    lon_e = lon_copies(2, pack_e, recv_w, recvx_w, east)
+    lon_w = lon_copies(5, pack_w, recv_e, recvx_e, west)
 
     def one(k, part):
-        def copy(i, src, dst, row):
-            return remote(src, dst, send_one.at[k + i], got_one.at[k + i], gx, row)
+        def copy(way, src, dst, row):
+            return remote(src, dst, send.at[way], got.at[k + way], gx, row)
 
         return (
             [
                 copy(0, xm.at[:, part, high, :], xm.at[:, part, from_s, :], north),
-                copy(1, xm.at[0, part, next_high, :], x1x.at[part, extra_s, :], north),
+                copy(0, xm.at[0, part, next_high, :], x1x.at[part, extra_s, :], north),
             ],
             [
-                copy(2, xm.at[:, part, low, :], xm.at[:, part, from_n, :], south),
-                copy(3, xm.at[0, part, next_low, :], x1x.at[part, extra_n, :], south),
+                copy(1, xm.at[:, part, low, :], xm.at[:, part, from_n, :], south),
+                copy(1, xm.at[0, part, next_low, :], x1x.at[part, extra_n, :], south),
             ],
         )
 
-    one_main = one(0, inside)
+    one_main = one(8, inside)
+    one_strips = (one(10, pl.ds(strips, per)), one(12, pl.ds(strips + per, per)))
 
     def start_up(up):
         @pl.when(has_n)
@@ -259,31 +269,35 @@
                 copy.start()
 
     def start_lon(copies):
-        copies[0].start()
+        copies[0][0].start()
         start_up(copies[1])
         start_down(copies[2])
 
-    def arrive(up, down):
+    def arrive(k, up, down):
         @pl.when(has_s)
         def _():
-            for copy in up:
-                copy.wait_recv()
+            wait_rows(rows_of(up), got.at[k])
 
         @pl.when(has_n)
         def _():
-            for copy in down:
-                copy.wait_recv()
-
-    def flush(up, down):
+            wait_rows(rows_of(down), got.at[k + 1])
+
+    def arrive_lon(k, copies):
+        wait_rows(rows_of(copies[0]), got.at[k])
+        arrive(k + 1, copies[1], copies[2])
+
+    def flush():
+        exchanges = ((up0, down0), one_main, *one_strips, lon_e[1:], lon_w[1:])
+
         @pl.when(has_n)
         def _():
-            for copy in up:
-                copy.wait_send()
+            wait_rows(sum(rows_of(up) for up, _ in exchanges), send.at[0])
 
         @pl.when(has_s)
         def _():
-            for copy in down:
-                copy.wait_send()
+            wait_rows(sum(rows_of(down) for _, down in exchanges), send.at[1])
+
+        wait_rows(rows_of(lon_e[0] + lon_w[0]), send.at[2])
 
     zero_ring = jnp.zeros((ring, lanes), jnp.float32)
     zero_tile = jnp.zeros((rows, lanes), jnp.float32)
@@ -333,13 +347,12 @@
             recvx_e[k, extra_s, :] = zero
             recvx_w[k, extra_s, :] = zero
 
-    for copy in loads:
-        copy.wait()
+    wait_rows(levels * FIELDS * rows, load_sem.at[0])
 
     def send_lat():
-        known(2)
+        known(2, 2)
         start_up(up0)
-        known(3)
+        known(3, 3)
         start_down(down0)
 
     @pl.when(jnp.logical_not(last_x))
@@ -399,12 +412,12 @@
 
     @pl.when(inner_x)
     def _():
-        known(1, 5, 7)
+        known(1, 1, 5, 7)
         start_lon(lon_w)
 
     @pl.when(jnp.logical_not(last_x))
     def _():
-        known(0, 4, 6)
+        known(0, 0, 4, 6)
         start_lon(lon_e)
 
     for f in range(FIELDS):
@@ -619,10 +632,10 @@
 
     @pl.when(first_x)
     def _():
-        known(1, 5, 7)
+        known(1, 1, 5, 7)
         start_lon(lon_w)
 
-    arrive(up0, down0)
+    arrive(0, up0, down0)
     each_main(prepare)
     sweeps(each_main, ad)
     each_main(close1)
@@ -660,10 +673,8 @@
             for k in range(2):
                 rawx[k, t] = jnp.where(where[:rows], turn(recvx[k], shift), rawx[k, t])
 
-    one_strips = (one(4, pl.ds(strips, per)), one(8, pl.ds(strips + per, per)))
-    for side, copies in ((1, lon_w), (0, lon_e)):
-        copies[0].wait_recv()
-        arrive(copies[1], copies[2])
+    for side, k, copies in ((1, 5, lon_w), (0, 2, lon_e)):
+        arrive_lon(k, copies)
         unpack(side)
         each = functools.partial(each_strip, side)
         each(prepare)
@@ -672,45 +683,45 @@
         start_up(one_strips[side][0])
         start_down(one_strips[side][1])
 
-    arrive(*one_main)
+    arrive(8, *one_main)
     each_main(second)
     sweeps(each_main, ad2)
     each_main(close2)
     each_main(finish)
 
+    east_edge = lane_row >= lanes - DEPTH
+
+    def merge_east():
+        for ref, out in ((x2, state_out), (mu2, adj_out), (res, resid_out)):
+            for l in range(levels):
+                j, g = l % per, l // per
+                e = turn(ref[strips + per + j][:rows], lanes - kept - GROUP * g)
+                out[l] = jnp.where(east_edge, e, ref[l + 1][:rows])
+
     for side in (1, 0):
-        arrive(*one_strips[side])
+        arrive(10 + 2 * side, *one_strips[side])
         each = functools.partial(each_strip, side)
         each(second)
         sweeps(each, ad2)
         each(close2)
         each(finish)
-
-    for copy in late_loads:
-        copy.wait()
+        if side == 1:
+            merge_east()
+            wait_rows(2 * levels * rows, load_sem.at[1])
 
     west_edge = lane_row < DEPTH
-    east_edge = lane_row >= lanes - DEPTH
-
-    def merged(ref, l):
+
+    def west_merged(ref, l, here):
         j, g = l % per, l // per
-        w = turn(ref[strips + j][:rows], -(GROUP * g + halo))
-        e = turn(ref[strips + per + j][:rows], lanes - kept - GROUP * g)
-        return jnp.where(west_edge, w, jnp.where(east_edge, e, ref[l + 1][:rows]))
+        return jnp.where(west_edge, turn(ref[strips + j][:rows], -(GROUP * g + halo)), here)
 
     for l in range(levels):
-        x = merged(x2, l)
+        x = west_merged(x2, l, state_out[l])
         state_out[l] = x
-        adj_out[l] = merged(mu2, l) + weight_ref[l] * (x - obs_ref[l])
-        resid_out[l] = merged(res, l)
-
-    flush(up0, down0)
-    flush(*one_main)
-    for copies in one_strips:
-        flush(*copies)
-    for copies in (lon_e, lon_w):
-        copies[0].wait_send()
-        flush(copies[1], copies[2])
+        adj_out[l] = west_merged(mu2, l, adj_out[l]) + late_ref[1, l] * (x - late_ref[0, l])
+        resid_out[l] = west_merged(res, l, resid_out[l])
+
+    flush()
 
 
 def hand_over(a, b, c, x, y, z, sem):
@@ -775,19 +786,15 @@
             + [full() for _ in range(11)]
             + [
                 buf(3, per, ring, lanes),
-                buf(levels, rows, lanes),
-                buf(levels, rows, lanes),
+                buf(2, levels, rows, lanes),
+                buf(FIELDS * levels * rows, lanes),
                 pltpu.SMEM((levels,), f32),
                 pltpu.SMEM((levels,), f32),
                 pltpu.SMEM((1,), jnp.int32),
-                dma(FIELDS + 5),
                 dma(5),
-                dma(5),
-                dma(8),
-                dma(8),
-                dma(12),
-                dma(12),
-                pltpu.SemaphoreType.REGULAR((8,)),
+                dma(3),
+                dma(14),
+                pltpu.SemaphoreType.REGULAR((4,)),
             ],
             compiler_params=pltpu.CompilerParams(
                 collective_id=0, has_side_effects=True, vmem_limit_bytes=67043328 - 3 * 4 * math.prod(out.shape)

time: 16.4 us -> 15.9 us (0.970)
  Pallas kernels: 14.9 us -> 14.5 us
    pallas_call x1, Pallas kernels: 14.2 us -> 13.8 us  [per_device(): pl.pallas_call(functools.partial(kernel, nx, ny), name='step_pair', out_s...]
where the time goes in v2:
time: 15.9 us; the launch traced here: 15.8 us
  Pallas kernels  14.5 us (91%)
  between operations  1.29 us (8%)
    pallas_call x1, Pallas kernels, per_device(): pl.pallas_call(functools.partial(kernel, nx, ny), name='step_pair', out_s...  13.8 us
    pallas_call x1, Pallas kernels, per_device(): pl.pallas_call(hand_over, name='hand_over', out_shape=(out, out, out), in...  0.7 us

profile of v2, /device:TPU:1, one launch (start us, length us, event | category | flops | bytes accessed | tf_op | source)
XLA Modules:
  0.0 15.8 jit_solution(3997840217787579184)
XLA Ops:
  1.3 13.8 %step_pair.1 = (f32[16,8,128]{2,1,0:T(8,128)S(1)}, f32[16,8,128]{2,1,0:T(8,128)S(1)}, f32[16,8,128]{2,1,0:T(8,128)S(1)}) custom-call(f32[16,8,128]{2,1,0:T(8,128)} %ckpt_h.1, f32[16,8,128]{2,1,0:T(8,128)} %traj_h.1, f32[16,8,128]{2,1,0:T(8,128)} %adjf_h.1, f32[16,8,128]{2,1,0:T(8,128)} %ed_h.1, f32[16,8,128]{2,1,0:T(8,128)} %nd_h.1, f32[16,8,128]{2,1,0:T(8,128)} %ew_h.1, ...), custom_call_target="tpu_custom_call" | custom-call | tf_op jit(solution)/shard_map/step_pair/pallas_call | solution.py:763
  15.1 0.7 %hand_over.1 = (f32[16,8,128]{2,1,0:T(8,128)}, f32[16,8,128]{2,1,0:T(8,128)}, f32[16,8,128]{2,1,0:T(8,128)}) custom-call(f32[16,8,128]{2,1,0:T(8,128)S(1)} %get-tuple-element.6.a, f32[16,8,128]{2,1,0:T(8,128)S(1)} %get-tuple-element.7.b, f32[16,8,128]{2,1,0:T(8,128)S(1)} %get-tuple-element.8.c), custom_call_target="tpu_custom_call" | custom-call | tf_op jit(solution)/shard_map/hand_over/pallas_call | solution.py:803

commit v3 on v2

--- a/solution.py
+++ b/solution.py
@@ -14,7 +14,8 @@
 RELAXATION = 0.7
 
 FIELDS = 8
-CKPT, SOURCE, ED, EW, ND, NW, TRAJ, ADJF = range(FIELDS)
+ND, NW, CKPT, ED, EW, SOURCE, TRAJ, ADJF = range(FIELDS)
+CORNER = 5
 
 DEPTH = OUTER * INNER + 1
 SLOT = DEPTH - 1
@@ -49,8 +50,6 @@
     pack_w,
     recv_e,
     recv_w,
-    recvx_e,
-    recvx_w,
     coef,
     cf,
     xm,
@@ -103,7 +102,7 @@
     inside = pl.ds(1, levels)
     main = pl.ds(0, rows)
 
-    order = (ckpt_h, source_h, ed_h, ew_h, nd_h, nw_h, traj_h, adjf_h)
+    order = (nd_h, nw_h, ckpt_h, ed_h, ew_h, source_h, traj_h, adjf_h)
     loads = [
         pltpu.make_async_copy(h, raw.at[f, inside, main, :], load_sem.at[0])
         for f, h in enumerate(order)
@@ -197,64 +196,60 @@
     from_s = pl.ds(ring - wide, wide)
     next_low = pl.ds(wide, 1)
     next_high = pl.ds(rows - wide - 1, 1)
+    near_low = pl.ds(0, wide - 1)
+    near_high = pl.ds(rows - wide + 1, wide - 1)
+    near_n = pl.ds(rows, wide - 1)
+    near_s = pl.ds(ring - wide + 1, wide - 1)
+    last_low = pl.ds(wide - 1, 1)
+    last_high = pl.ds(rows - wide, 1)
+    last_n = pl.ds(rows + wide - 1, 1)
+    last_s = pl.ds(ring - wide, 1)
     extra_n = pl.ds(wide - 1, 1)
     extra_s = pl.ds(wide, 1)
 
     faces = pl.ds(ND, 2)
 
+    def copy(k, src, dst, column, row):
+        return remote(src, dst, send.at[0], got.at[k], column, row)
+
     up0 = [
-        remote(raw.at[:, inside, high, :], raw.at[:, inside, from_s, :], send.at[0], got.at[0], gx, north),
-        remote(
-            raw.at[faces, inside, next_high, :], rawx.at[:, inside, extra_s, :], send.at[0], got.at[0], gx, north
-        ),
+        copy(0, raw.at[:, inside, high, :], raw.at[:, inside, from_s, :], gx, north),
+        copy(0, raw.at[faces, inside, next_high, :], rawx.at[:, inside, extra_s, :], gx, north),
     ]
-    down0 = [
-        remote(raw.at[:, inside, low, :], raw.at[:, inside, from_n, :], send.at[1], got.at[1], gx, south)
-    ]
-
-    def lon_copies(k, pack, recv, recvx, column):
+    down0 = [copy(0, raw.at[:, inside, low, :], raw.at[:, inside, from_n, :], gx, south)]
+
+    some = pl.ds(0, CORNER)
+
+    def lon_copies(k, pack, recv, column):
         return (
-            [remote(pack, recv.at[:, main, :], send.at[2], got.at[k], column, gy)],
+            [copy(k, pack, recv.at[:, main, :], column, gy)],
             [
-                remote(
-                    pack.at[:, high, :], recv.at[:, from_s, :], send.at[0], got.at[k + 1], column, north
-                ),
-                remote(
-                    pack.at[faces, next_high, :],
-                    recvx.at[:, extra_s, :],
-                    send.at[0],
-                    got.at[k + 1],
-                    column,
-                    north,
-                ),
+                copy(k, pack.at[:, near_high, :], recv.at[:, near_s, :], column, north),
+                copy(k, pack.at[some, last_high, :], recv.at[some, last_s, :], column, north),
             ],
             [
-                remote(
-                    pack.at[:, low, :], recv.at[:, from_n, :], send.at[1], got.at[k + 2], column, south
-                )
+                copy(k, pack.at[:, near_low, :], recv.at[:, near_n, :], column, south),
+                copy(k, pack.at[some, last_low, :], recv.at[some, last_n, :], column, south),
             ],
         )
 
-    lon_e = lon_copies(2, pack_e, recv_w, recvx_w, east)
-    lon_w = lon_copies(5, pack_w, recv_e, recvx_e, west)
+    lon_e = lon_copies(1, pack_e, recv_w, east)
+    lon_w = lon_copies(2, pack_w, recv_e, west)
 
     def one(k, part):
-        def copy(way, src, dst, row):
-            return remote(src, dst, send.at[way], got.at[k + way], gx, row)
-
         return (
             [
-                copy(0, xm.at[:, part, high, :], xm.at[:, part, from_s, :], north),
-                copy(0, xm.at[0, part, next_high, :], x1x.at[part, extra_s, :], north),
+                copy(k, xm.at[:, part, high, :], xm.at[:, part, from_s, :], gx, north),
+                copy(k, xm.at[0, part, next_high, :], x1x.at[part, extra_s, :], gx, north),
             ],
             [
-                copy(1, xm.at[:, part, low, :], xm.at[:, part, from_n, :], south),
-                copy(1, xm.at[0, part, next_low, :], x1x.at[part, extra_n, :], south),
+                copy(k, xm.at[:, part, low, :], xm.at[:, part, from_n, :], gx, south),
+                copy(k, xm.at[0, part, next_low, :], x1x.at[part, extra_n, :], gx, south),
             ],
         )
 
-    one_main = one(8, inside)
-    one_strips = (one(10, pl.ds(strips, per)), one(12, pl.ds(strips + per, per)))
+    one_main = one(3, inside)
+    one_strips = (one(4, pl.ds(strips, per)), one(5, pl.ds(strips + per, per)))
 
     def start_up(up):
         @pl.when(has_n)
@@ -273,31 +268,37 @@
         start_up(copies[1])
         start_down(copies[2])
 
+    def wait_all(always, up, down, with_up, with_down, sem):
+        n, n_up, n_down = rows_of(always), rows_of(up), rows_of(down)
+        cases = (
+            (jnp.logical_and(with_up, with_down), n + n_up + n_down),
+            (jnp.logical_and(with_up, jnp.logical_not(with_down)), n + n_up),
+            (jnp.logical_and(with_down, jnp.logical_not(with_up)), n + n_down),
+            (jnp.logical_not(jnp.logical_or(with_up, with_down)), n),
+        )
+        for case, total in cases:
+            if total:
+
+                @pl.when(case)
+                def _():
+                    wait_rows(total, sem)
+
     def arrive(k, up, down):
-        @pl.when(has_s)
-        def _():
-            wait_rows(rows_of(up), got.at[k])
-
-        @pl.when(has_n)
-        def _():
-            wait_rows(rows_of(down), got.at[k + 1])
+        wait_all([], up, down, has_s, has_n, got.at[k])
 
     def arrive_lon(k, copies):
-        wait_rows(rows_of(copies[0]), got.at[k])
-        arrive(k + 1, copies[1], copies[2])
+        wait_all(*copies, has_s, has_n, got.at[k])
 
     def flush():
         exchanges = ((up0, down0), one_main, *one_strips, lon_e[1:], lon_w[1:])
-
-        @pl.when(has_n)
-        def _():
-            wait_rows(sum(rows_of(up) for up, _ in exchanges), send.at[0])
-
-        @pl.when(has_s)
-        def _():
-            wait_rows(sum(rows_of(down) for _, down in exchanges), send.at[1])
-
-        wait_rows(rows_of(lon_e[0] + lon_w[0]), send.at[2])
+        wait_all(
+            lon_e[0] + lon_w[0],
+            [copy for up, _ in exchanges for copy in up],
+            [copy for _, down in exchanges for copy in down],
+            has_n,
+            has_s,
+            send.at[0],
+        )
 
     zero_ring = jnp.zeros((ring, lanes), jnp.float32)
     zero_tile = jnp.zeros((rows, lanes), jnp.float32)
@@ -344,8 +345,6 @@
         for k in range(2):
             for t in range(1, levels + 1):
                 rawx[k, t, extra_s, :] = zero
-            recvx_e[k, extra_s, :] = zero
-            recvx_w[k, extra_s, :] = zero
 
     wait_rows(levels * FIELDS * rows, load_sem.at[0])
 
@@ -657,10 +656,7 @@
             for j in range(per):
                 rawx[k, strips + per * side + j] = gather(lambda l: rawx[k, l + 1], group_row, side, j)
     def unpack(side):
-        recv, recvx, where, lead, nines = (
-            (recv_w, recvx_w, from_w, 1, NINTH),
-            (recv_e, recvx_e, from_e, kept, (CKPT,)),
-        )[side]
+        recv, where, lead, nines = ((recv_w, from_w, 1, NINTH), (recv_e, from_e, kept, (CKPT,)))[side]
         beyond = spot == (0 if side == 0 else GROUP - 1)
         for j in range(per):
             t = strips + per * side + j
@@ -670,10 +666,8 @@
                 if f in nines:
                     tile = jnp.where(beyond, turn(recv[FIELDS], shift + nines.index(f)), tile)
                 raw[f, t] = tile
-            for k in range(2):
-                rawx[k, t] = jnp.where(where[:rows], turn(recvx[k], shift), rawx[k, t])
-
-    for side, k, copies in ((1, 5, lon_w), (0, 2, lon_e)):
+
+    for side, k, copies in ((1, 2, lon_w), (0, 1, lon_e)):
         arrive_lon(k, copies)
         unpack(side)
         each = functools.partial(each_strip, side)
@@ -683,7 +677,7 @@
         start_up(one_strips[side][0])
         start_down(one_strips[side][1])
 
-    arrive(8, *one_main)
+    arrive(3, *one_main)
     each_main(second)
     sweeps(each_main, ad2)
     each_main(close2)
@@ -699,7 +693,7 @@
                 out[l] = jnp.where(east_edge, e, ref[l + 1][:rows])
 
     for side in (1, 0):
-        arrive(10 + 2 * side, *one_strips[side])
+        arrive(4 + side, *one_strips[side])
         each = functools.partial(each_strip, side)
         each(second)
         sweeps(each, ad2)
@@ -773,8 +767,6 @@
                 buf(FIELDS + 1, rows, lanes),
                 buf(FIELDS + 1, ring, lanes),
                 buf(FIELDS + 1, ring, lanes),
-                buf(2, rows, lanes),
-                buf(2, rows, lanes),
                 buf(10, tiles, ring, lanes),
                 full(),
                 buf(2, tiles, ring, lanes),
@@ -787,13 +779,13 @@
             + [
                 buf(3, per, ring, lanes),
                 buf(2, levels, rows, lanes),
-                buf(FIELDS * levels * rows, lanes),
+                buf(2 * FIELDS * levels * rows, lanes),
                 pltpu.SMEM((levels,), f32),
                 pltpu.SMEM((levels,), f32),
                 pltpu.SMEM((1,), jnp.int32),
                 dma(5),
-                dma(3),
-                dma(14),
+                dma(1),
+                dma(6),
                 pltpu.SemaphoreType.REGULAR((4,)),
             ],
             compiler_params=pltpu.CompilerParams(

time: 15.9 us -> 15.8 us (level)
  no operation moved by 1% of the time
where the time goes in v3:
time: 15.8 us; the launch traced here: 15.7 us
  Pallas kernels  14.4 us (91%)
  between operations  1.29 us (8%)
    pallas_call x1, Pallas kernels, per_device(): pl.pallas_call(functools.partial(kernel, nx, ny), name='step_pair', out_s...  13.7 us
    pallas_call x1, Pallas kernels, per_device(): pl.pallas_call(hand_over, name='hand_over', out_shape=(out, out, out), in...  0.7 us

profile of v3, /device:TPU:1, one launch (start us, length us, event | category | flops | bytes accessed | tf_op | source)
XLA Modules:
  0.0 15.7 jit_solution(10379737296250460508)
XLA Ops:
  1.3 13.7 %step_pair.1 = (f32[16,8,128]{2,1,0:T(8,128)S(1)}, f32[16,8,128]{2,1,0:T(8,128)S(1)}, f32[16,8,128]{2,1,0:T(8,128)S(1)}) custom-call(f32[16,8,128]{2,1,0:T(8,128)} %ckpt_h.1, f32[16,8,128]{2,1,0:T(8,128)} %traj_h.1, f32[16,8,128]{2,1,0:T(8,128)} %adjf_h.1, f32[16,8,128]{2,1,0:T(8,128)} %ed_h.1, f32[16,8,128]{2,1,0:T(8,128)} %nd_h.1, f32[16,8,128]{2,1,0:T(8,128)} %ew_h.1, ...), custom_call_target="tpu_custom_call" | custom-call | tf_op jit(solution)/shard_map/step_pair/pallas_call | solution.py:757
  15.0 0.7 %hand_over.1 = (f32[16,8,128]{2,1,0:T(8,128)}, f32[16,8,128]{2,1,0:T(8,128)}, f32[16,8,128]{2,1,0:T(8,128)}) custom-call(f32[16,8,128]{2,1,0:T(8,128)S(1)} %get-tuple-element.6.a, f32[16,8,128]{2,1,0:T(8,128)S(1)} %get-tuple-element.7.b, f32[16,8,128]{2,1,0:T(8,128)S(1)} %get-tuple-element.8.c), custom_call_target="tpu_custom_call" | custom-call | tf_op jit(solution)/shard_map/hand_over/pallas_call | solution.py:795

commit v4 on v3

--- a/solution.py
+++ b/solution.py
@@ -15,6 +15,7 @@
 
 FIELDS = 8
 ND, NW, CKPT, ED, EW, SOURCE, TRAJ, ADJF = range(FIELDS)
+FORWARD = 6
 CORNER = 5
 
 DEPTH = OUTER * INNER + 1
@@ -117,6 +118,9 @@
         pltpu.make_async_copy(step_h, step_ref, load_sem.at[4]),
     ]
 
+    for copy in loads:
+        copy.start()
+
     barrier = pltpu.get_barrier_semaphore()
     odd_x = lax.rem(gx, 2) == 1
     odd_y = lax.rem(gy, 2) == 1
@@ -148,8 +152,6 @@
                 barrier, inc=1, device_id={"gx": column, "gy": row}, device_id_type=MESH
             )
 
-    for copy in loads + scalar_loads + late_loads:
-        copy.start()
 
     @pl.when(behind > 0)
     def _():
@@ -212,23 +214,28 @@
     def copy(k, src, dst, column, row):
         return remote(src, dst, send.at[0], got.at[k], column, row)
 
+    fwd = pl.ds(0, FORWARD)
+    adj = pl.ds(FORWARD, FIELDS - FORWARD)
     up0 = [
-        copy(0, raw.at[:, inside, high, :], raw.at[:, inside, from_s, :], gx, north),
+        copy(0, raw.at[fwd, inside, high, :], raw.at[fwd, inside, from_s, :], gx, north),
         copy(0, raw.at[faces, inside, next_high, :], rawx.at[:, inside, extra_s, :], gx, north),
     ]
-    down0 = [copy(0, raw.at[:, inside, low, :], raw.at[:, inside, from_n, :], gx, south)]
-
+    down0 = [copy(0, raw.at[fwd, inside, low, :], raw.at[fwd, inside, from_n, :], gx, south)]
+    up0a = [copy(6, raw.at[adj, inside, near_high, :], raw.at[adj, inside, near_s, :], gx, north)]
+    down0a = [copy(6, raw.at[adj, inside, near_low, :], raw.at[adj, inside, near_n, :], gx, south)]
+
+    every = pl.ds(0, FIELDS)
     some = pl.ds(0, CORNER)
 
     def lon_copies(k, pack, recv, column):
         return (
             [copy(k, pack, recv.at[:, main, :], column, gy)],
             [
-                copy(k, pack.at[:, near_high, :], recv.at[:, near_s, :], column, north),
+                copy(k, pack.at[every, near_high, :], recv.at[every, near_s, :], column, north),
                 copy(k, pack.at[some, last_high, :], recv.at[some, last_s, :], column, north),
             ],
             [
-                copy(k, pack.at[:, near_low, :], recv.at[:, near_n, :], column, south),
+                copy(k, pack.at[every, near_low, :], recv.at[every, near_n, :], column, south),
                 copy(k, pack.at[some, last_low, :], recv.at[some, last_n, :], column, south),
             ],
         )
@@ -248,7 +255,20 @@
             ],
         )
 
-    one_main = one(3, inside)
+    one_x = (
+        [
+            copy(3, xm.at[0, inside, high, :], xm.at[0, inside, from_s, :], gx, north),
+            copy(3, xm.at[0, inside, next_high, :], x1x.at[inside, extra_s, :], gx, north),
+        ],
+        [
+            copy(3, xm.at[0, inside, low, :], xm.at[0, inside, from_n, :], gx, south),
+            copy(3, xm.at[0, inside, next_low, :], x1x.at[inside, extra_n, :], gx, south),
+        ],
+    )
+    one_m = (
+        [copy(7, xm.at[1, inside, high, :], xm.at[1, inside, from_s, :], gx, north)],
+        [copy(7, xm.at[1, inside, low, :], xm.at[1, inside, from_n, :], gx, south)],
+    )
     one_strips = (one(4, pl.ds(strips, per)), one(5, pl.ds(strips + per, per)))
 
     def start_up(up):
@@ -290,7 +310,7 @@
         wait_all(*copies, has_s, has_n, got.at[k])
 
     def flush():
-        exchanges = ((up0, down0), one_main, *one_strips, lon_e[1:], lon_w[1:])
+        exchanges = ((up0, down0), (up0a, down0a), one_x, one_m, *one_strips, lon_e[1:], lon_w[1:])
         wait_all(
             lon_e[0] + lon_w[0],
             [copy for up, _ in exchanges for copy in up],
@@ -350,9 +370,12 @@
 
     def send_lat():
         known(2, 2)
-        start_up(up0)
+        start_up(up0 + up0a)
         known(3, 3)
-        start_down(down0)
+        start_down(down0 + down0a)
+
+    for copy in scalar_loads + late_loads:
+        copy.start()
 
     @pl.when(jnp.logical_not(last_x))
     def _():
@@ -388,7 +411,7 @@
         return k % per + per * (k // per)
 
     nine = None
-    for f in range(FIELDS):
+    for f in sorted(range(FIELDS), key=lambda f: f not in NINTH):
         if f in NINTH:
             pack_e[f], beside = slots(f, SLOT, (0, 1))
             i = NINTH.index(f)
@@ -588,6 +611,11 @@
         for k, value in enumerate((a, b, a_w, b_w, an, bn, an_s, bn_s, diag, total)):
             coef[k, c.t] = value
         cf[c.t] = raw[CKPT, c.t] + raw[SOURCE, c.t] * c.heat
+        resid_forward(c, raw.at[CKPT])
+
+    def prepare_adjoint(c):
+        _, _, damp = c.terms()
+        diag, total = coef[8, c.t], coef[9, c.t]
         t = jnp.tanh(raw[TRAJ, c.t])
         local = damp * (1.0 - t * t)
         w = RELAXATION / (total + local)
@@ -596,7 +624,6 @@
         ag[c.t] = 1.0 - w * (diag + local)
         ad[c.t] = start_delta
         aa[c.t] = start_delta
-        resid_forward(c, raw.at[CKPT])
 
     pairs = ((fa, fb, aa, ab), (fb, fa, ab, aa))
     last = pairs[(INNER - 2) % 2]
@@ -611,13 +638,24 @@
 
             each(body)
 
-    def close1(c):
+    def close_x(c):
         xm[0, c.t, :rows, :] = raw[CKPT, c.t, :rows, :] + lin_forward(c, last[0])[:rows]
+
+    def close_m(c):
         xm[1, c.t, :rows, :] = lin_adjoint(c, last[2], ad)[:rows]
 
-    def second(c):
+    def second_x(c):
         resid_forward(c, xm.at[0], x1x)
+
+    def second_m(c):
         resid_adjoint(c, xm.at[1])
+
+    def both(first, then):
+        def body(c):
+            first(c)
+            then(c)
+
+        return body
 
     def close2(c):
         x2[c.t] = xm[0, c.t] + lin_forward(c, last[0])
@@ -636,10 +674,15 @@
 
     arrive(0, up0, down0)
     each_main(prepare)
+    arrive(6, up0a, down0a)
+    each_main(prepare_adjoint)
     sweeps(each_main, ad)
-    each_main(close1)
-    start_up(one_main[0])
-    start_down(one_main[1])
+    each_main(close_x)
+    start_down(one_x[1])
+    start_up(one_x[0])
+    each_main(close_m)
+    start_down(one_m[1])
+    start_up(one_m[0])
 
     spot = lane_ring % GROUP
     from_w = (spot > 0) & (spot < halo)
@@ -671,14 +714,16 @@
         arrive_lon(k, copies)
         unpack(side)
         each = functools.partial(each_strip, side)
-        each(prepare)
+        each(both(prepare, prepare_adjoint))
         sweeps(each, ad)
-        each(close1)
+        each(both(close_x, close_m))
+        start_down(one_strips[side][1])
         start_up(one_strips[side][0])
-        start_down(one_strips[side][1])
-
-    arrive(3, *one_main)
-    each_main(second)
+
+    arrive(3, *one_x)
+    each_main(second_x)
+    arrive(7, *one_m)
+    each_main(second_m)
     sweeps(each_main, ad2)
     each_main(close2)
     each_main(finish)
@@ -695,7 +740,7 @@
     for side in (1, 0):
         arrive(4 + side, *one_strips[side])
         each = functools.partial(each_strip, side)
-        each(second)
+        each(both(second_x, second_m))
         sweeps(each, ad2)
         each(close2)
         each(finish)
@@ -785,7 +830,7 @@
                 pltpu.SMEM((1,), jnp.int32),
                 dma(5),
                 dma(1),
-                dma(6),
+                dma(8),
                 pltpu.SemaphoreType.REGULAR((4,)),
             ],
             compiler_params=pltpu.CompilerParams(

time: 15.8 us -> 15.7 us (level)
  no operation moved by 1% of the time
where the time goes in v4:
time: 15.7 us; the launch traced here: 15.6 us
  Pallas kernels  14.3 us (91%)
  between operations  1.29 us (8%)
    pallas_call x1, Pallas kernels, per_device(): pl.pallas_call(functools.partial(kernel, nx, ny), name='step_pair', out_s...  13.6 us
    pallas_call x1, Pallas kernels, per_device(): pl.pallas_call(hand_over, name='hand_over', out_shape=(out, out, out), in...  0.7 us

profile of v4, /device:TPU:1, one launch (start us, length us, event | category | flops | bytes accessed | tf_op | source)
XLA Modules:
  0.0 15.6 jit_solution(6153627967313061999)
XLA Ops:
  1.3 13.6 %step_pair.1 = (f32[16,8,128]{2,1,0:T(8,128)S(1)}, f32[16,8,128]{2,1,0:T(8,128)S(1)}, f32[16,8,128]{2,1,0:T(8,128)S(1)}) custom-call(f32[16,8,128]{2,1,0:T(8,128)} %ckpt_h.1, f32[16,8,128]{2,1,0:T(8,128)} %traj_h.1, f32[16,8,128]{2,1,0:T(8,128)} %adjf_h.1, f32[16,8,128]{2,1,0:T(8,128)} %ed_h.1, f32[16,8,128]{2,1,0:T(8,128)} %nd_h.1, f32[16,8,128]{2,1,0:T(8,128)} %ew_h.1, ...), custom_call_target="tpu_custom_call" | custom-call | tf_op jit(solution)/shard_map/step_pair/pallas_call | solution.py:802
  14.9 0.7 %hand_over.1 = (f32[16,8,128]{2,1,0:T(8,128)}, f32[16,8,128]{2,1,0:T(8,128)}, f32[16,8,128]{2,1,0:T(8,128)}) custom-call(f32[16,8,128]{2,1,0:T(8,128)S(1)} %get-tuple-element.6.a, f32[16,8,128]{2,1,0:T(8,128)S(1)} %get-tuple-element.7.b, f32[16,8,128]{2,1,0:T(8,128)S(1)} %get-tuple-element.8.c), custom_call_target="tpu_custom_call" | custom-call | tf_op jit(solution)/shard_map/hand_over/pallas_call | solution.py:840

commit v5 on v4

--- a/solution.py
+++ b/solution.py
@@ -126,6 +126,7 @@
     odd_y = lax.rem(gy, 2) == 1
     even_y = jnp.logical_not(odd_y)
     inner_x = jnp.logical_not(first_x)
+    before_lat = odd_y != last_x
     before_e = jnp.logical_or(last_x, odd_x)
     before_w = jnp.logical_and(inner_x, odd_x)
     before_de = jnp.logical_or(last_x, even_y)
@@ -133,8 +134,8 @@
     neighbours = (
         (east, gy, True, before_e),
         (west, gy, True, before_w),
-        (gx, north, has_n, odd_y),
-        (gx, south, has_s, odd_y),
+        (gx, north, has_n, before_lat),
+        (gx, south, has_s, before_lat),
         (east, north, has_n, before_de),
         (west, north, has_n, before_dw),
         (east, south, has_s, before_de),

time: 15.7 us -> 15.5 us (0.987); the launches traced: 15.6 us -> 15.2 us
  Pallas kernels: 14.3 us -> 13.9 us
    pallas_call x1, Pallas kernels: 13.6 us -> 13.2 us  [per_device(): pl.pallas_call(functools.partial(kernel, nx, ny), name='step_pair', out_s...]
where the time goes in v5:
time: 15.5 us; the launch traced here: 15.2 us
  Pallas kernels  13.9 us (90%)
  between operations  1.29 us (8%)
    pallas_call x1, Pallas kernels, per_device(): pl.pallas_call(functools.partial(kernel, nx, ny), name='step_pair', out_s...  13.2 us
    pallas_call x1, Pallas kernels, per_device(): pl.pallas_call(hand_over, name='hand_over', out_shape=(out, out, out), in...  0.7 us

profile of v5, /device:TPU:1, one launch (start us, length us, event | category | flops | bytes accessed | tf_op | source)
XLA Modules:
  0.0 15.2 jit_solution(13621694781998846769)
XLA Ops:
  1.3 13.2 %step_pair.1 = (f32[16,8,128]{2,1,0:T(8,128)S(1)}, f32[16,8,128]{2,1,0:T(8,128)S(1)}, f32[16,8,128]{2,1,0:T(8,128)S(1)}) custom-call(f32[16,8,128]{2,1,0:T(8,128)} %ckpt_h.1, f32[16,8,128]{2,1,0:T(8,128)} %traj_h.1, f32[16,8,128]{2,1,0:T(8,128)} %adjf_h.1, f32[16,8,128]{2,1,0:T(8,128)} %ed_h.1, f32[16,8,128]{2,1,0:T(8,128)} %nd_h.1, f32[16,8,128]{2,1,0:T(8,128)} %ew_h.1, ...), custom_call_target="tpu_custom_call" | custom-call | tf_op jit(solution)/shard_map/step_pair/pallas_call | solution.py:803
  14.5 0.7 %hand_over.1 = (f32[16,8,128]{2,1,0:T(8,128)}, f32[16,8,128]{2,1,0:T(8,128)}, f32[16,8,128]{2,1,0:T(8,128)}) custom-call(f32[16,8,128]{2,1,0:T(8,128)S(1)} %get-tuple-element.6.a, f32[16,8,128]{2,1,0:T(8,128)S(1)} %get-tuple-element.7.b, f32[16,8,128]{2,1,0:T(8,128)S(1)} %get-tuple-element.8.c), custom_call_target="tpu_custom_call" | custom-call | tf_op jit(solution)/shard_map/hand_over/pallas_call | solution.py:841

commit v6 on v5

--- a/solution.py
+++ b/solution.py
@@ -144,7 +144,8 @@
     answer_to = (1, 0, 3, 2, 1, 0, 1, 0)
 
     behind = 0
-    for column, row, there, before in neighbours:
+    for k in (7, 5, 1, 2, 3, 0, 4, 6):
+        column, row, there, before = neighbours[k]
         behind = behind + jnp.logical_and(there, before).astype(jnp.int32)
 
         @pl.when(jnp.logical_and(there, jnp.logical_not(before)))

time: 15.5 us -> 15.4 us (level)
  no operation moved by 1% of the time
where the time goes in v6:
time: 15.4 us; the launch traced here: 15.1 us
  Pallas kernels  13.8 us (90%)
  between operations  1.29 us (8%)
    pallas_call x1, Pallas kernels, per_device(): pl.pallas_call(functools.partial(kernel, nx, ny), name='step_pair', out_s...  13.1 us
    pallas_call x1, Pallas kernels, per_device(): pl.pallas_call(hand_over, name='hand_over', out_shape=(out, out, out), in...  0.7 us

profile of v6, /device:TPU:1, one launch (start us, length us, event | category | flops | bytes accessed | tf_op | source)
XLA Modules:
  0.0 15.1 jit_solution(13221650217311221559)
XLA Ops:
  1.3 13.1 %step_pair.1 = (f32[16,8,128]{2,1,0:T(8,128)S(1)}, f32[16,8,128]{2,1,0:T(8,128)S(1)}, f32[16,8,128]{2,1,0:T(8,128)S(1)}) custom-call(f32[16,8,128]{2,1,0:T(8,128)} %ckpt_h.1, f32[16,8,128]{2,1,0:T(8,128)} %traj_h.1, f32[16,8,128]{2,1,0:T(8,128)} %adjf_h.1, f32[16,8,128]{2,1,0:T(8,128)} %ed_h.1, f32[16,8,128]{2,1,0:T(8,128)} %nd_h.1, f32[16,8,128]{2,1,0:T(8,128)} %ew_h.1, ...), custom_call_target="tpu_custom_call" | custom-call | tf_op jit(solution)/shard_map/step_pair/pallas_call | solution.py:804
  14.4 0.7 %hand_over.1 = (f32[16,8,128]{2,1,0:T(8,128)}, f32[16,8,128]{2,1,0:T(8,128)}, f32[16,8,128]{2,1,0:T(8,128)}) custom-call(f32[16,8,128]{2,1,0:T(8,128)S(1)} %get-tuple-element.6.a, f32[16,8,128]{2,1,0:T(8,128)S(1)} %get-tuple-element.7.b, f32[16,8,128]{2,1,0:T(8,128)S(1)} %get-tuple-element.8.c), custom_call_target="tpu_custom_call" | custom-call | tf_op jit(solution)/shard_map/hand_over/pallas_call | solution.py:842
